TPU v7x, 32 devices: a whole 2x2x4 slice. The times are simulated.
32 devices in a mesh: dp: 8 (over y, x, core), expert: 4 (over z).
Axes of the slice: x: 2, y: 2, z: 4, core: 2. Of those that a mesh axis runs over, the one named last changes fastest.
Arguments:
- hidden_states: bfloat16 [4, 8192, 4096], P(None, ('dp', 'expert')), may hold values from -8 to 8
- router_weight: bfloat16 [4, 8, 4096], replicated, may hold values from -0.125 to 0.125
- expert_ids: int32 [4, 8192, 2], P(None, ('dp', 'expert')), may hold values from 0 to 7, as said below
Outputs:
- router_grad: float32 [4, 8, 4096], P(None, None, 'dp')
- losses: float32 [4, 2], replicated
Inputs may be any that keep to these rules, and one draw needn't show every extreme that they name: `expert_ids`: each token names 2 different experts in each layer.
All inputs are finite; a program needn't handle non-finite values.
Results may differ from a plain program's by a relative error of at most 0.0018.
Values sent between devices are 32-bit elements; how exact they have to be, the bound alone decides.
A program may use at most 64 MiB of HBM per device.

v0:
```python
import jax
import jax.numpy as jnp
from jax import lax
from jax.sharding import PartitionSpec as P

balance_coef = 0.02
zloss_coef = 0.001


def local_counts(chosen, experts):
    labels = jnp.arange(experts, dtype=jnp.int32)[:, None]
    counts = jnp.zeros((experts,), jnp.float32)
    for slot in range(chosen.shape[1]):
        counts = counts + jnp.sum((chosen[:, slot][None, :] == labels).astype(jnp.float32), axis=1)
    return counts


def on_device(hidden_states, router_weight, expert_ids):
    layers = hidden_states.shape[0]
    rows = hidden_states.shape[1]
    experts = router_weight.shape[1]
    picks = expert_ids.shape[2]
    tokens_all = rows * lax.axis_size("dp") * lax.axis_size("expert")
    terms = []
    count_list = []
    prob_sums = []
    square_sums = []
    for layer in range(layers):
        states = hidden_states[layer]
        logits = lax.dot_general(
            router_weight[layer],
            states,
            (((1,), (1,)), ((), ())),
            preferred_element_type=jnp.float32,
        )
        expo = jnp.exp(logits)
        total = jnp.sum(expo, axis=0)
        probs = expo / total[None, :]
        lse = jnp.log(total)
        prob_sums.append(jnp.sum(probs, axis=1))
        square_sums.append(jnp.sum(lse * lse))
        counts = lax.psum(local_counts(expert_ids[layer], experts), ("dp", "expert"))
        count_list.append(counts)
        share = counts / (tokens_all * picks)
        pull = balance_coef * experts * share
        mixed = jnp.sum(probs * pull[:, None], axis=0)
        dlogits = probs * (pull[:, None] - mixed[None, :]) + 2.0 * zloss_coef * lse[None, :] * probs
        dlogits = dlogits.astype(jnp.bfloat16)
        term = jnp.dot(dlogits, states, preferred_element_type=jnp.float32)
        terms.append(term)
    columns = lax.psum_scatter(jnp.stack(terms), "dp", scatter_dimension=2, tiled=True)
    router_grad = lax.psum(columns, "expert")
    prob_total, square_total = lax.psum(
        (jnp.stack(prob_sums), jnp.stack(square_sums)), ("dp", "expert")
    )
    share_table = jnp.stack(count_list) / (tokens_all * picks)
    balance = experts * jnp.sum(share_table * prob_total / tokens_all, axis=1)
    zloss = square_total / tokens_all
    return (router_grad, jnp.stack([balance, zloss], axis=-1))


def solution(mesh):
    in_specs = (P(None, ("dp", "expert"), None), P(), P(None, ("dp", "expert"), None))
    out_specs = (P(None, None, "dp"), P())
    return jax.shard_map(
        on_device, mesh=mesh, in_specs=in_specs, out_specs=out_specs, check_vma=False
    )
```

profile of v0, /device:TPU:0, one launch (start us, length us, event | category | flops | bytes accessed | tf_op | source)
XLA Modules:
  0.0 158.2 jit_solution(140643967143512886)
XLA Ops:
  7.2 2.3 %fusion.65 = (f32[256]{0:T(256)S(1)}, f32[8,256]{1,0:T(8,128)S(1)}) fusion(bf16[4,256,4096]{2,1,0:T(8,128)(2,1)} %param.3, bf16[4,8,4096]{2,1,0:T(8,128)(2,1)} %param.4), kind=kOutput, calls=%fused_computation.112 | convolution fusion | flops 16779008 | bytes 2171904 | tf_op jit(solution)/shard_map/dot_general | solution.py:30
  9.5 2.3 %fusion.66 = (f32[256]{0:T(256)S(1)}, f32[8,256]{1,0:T(8,128)S(1)}) fusion(bf16[4,256,4096]{2,1,0:T(8,128)(2,1)} %param.3, bf16[4,8,4096]{2,1,0:T(8,128)(2,1)} %param.4), kind=kOutput, calls=%fused_computation.113 | convolution fusion | flops 16779008 | bytes 2171904 | tf_op jit(solution)/shard_map/dot_general | solution.py:30
  11.8 2.3 %fusion.63 = (f32[256]{0:T(256)S(1)}, f32[8,256]{1,0:T(8,128)S(1)}) fusion(bf16[4,256,4096]{2,1,0:T(8,128)(2,1)} %param.3, bf16[4,8,4096]{2,1,0:T(8,128)(2,1)} %param.4), kind=kOutput, calls=%fused_computation.110 | convolution fusion | flops 16779008 | bytes 2171904 | tf_op jit(solution)/shard_map/dot_general | solution.py:30
  14.1 0.7 slice_bitcast_fusion.3
  14.9 0.1 convert_reduce_fusion.6
  15.0 0.1 convert_reduce_fusion.7
  15.1 0.1 convert_reduce_fusion.4
  15.2 0.1 convert_reduce_fusion.5
  15.4 0.1 convert_reduce_fusion
  15.5 0.1 convert_reduce_fusion.1
  15.6 0.1 convert_reduce_fusion.2
  15.7 0.1 convert_reduce_fusion.3
  15.9 2.3 %fusion.64 = (f32[256]{0:T(256)S(1)}, f32[8,256]{1,0:T(8,128)S(1)}) fusion(bf16[4,256,4096]{2,1,0:T(8,128)(2,1)} %param.3, bf16[4,8,4096]{2,1,0:T(8,128)(2,1)} %param.4), kind=kOutput, calls=%fused_computation.111 | convolution fusion | flops 16779008 | bytes 2171904 | tf_op jit(solution)/shard_map/dot_general | solution.py:30
  18.2 42.0 %all-reduce.1 = (f32[8]{0:T(128)S(1)}, f32[8]{0:T(128)S(1)}, f32[8]{0:T(128)S(1)}, f32[8]{0:T(128)S(1)}) all-reduce(f32[8]{0:T(128)S(1)} %add.46, f32[8]{0:T(128)S(1)} %add.44, f32[8]{0:T(128)S(1)} %add.42, f32[8]{0:T(128)S(1)} %add.40), channel_id=1, replica_groups=mesh['dp'=8,'expert'=4] {'dp','expert'}, use_global_device_ids=true, to_apply=%region_18.0 | all-reduce | flops 32 | bytes 256 | tf_op jit(solution)/shard_map/psum | solution.py:42
  60.2 0.6 multiply_reduce_fusion.6
  60.8 0.7 multiply_reduce_fusion.7
  61.5 0.6 multiply_reduce_fusion.4
  62.1 0.6 multiply_reduce_fusion.5
  62.7 0.2 fusion.55
  62.9 2.0 %convolution_bitcast_fusion.3 = f32[1,8,4096]{2,1,0:T(8,128)S(1)} fusion(bf16[4,256,4096]{2,1,0:T(8,128)(2,1)} %param.3, f32[256]{0:T(256)S(1)} %get-tuple-element.29, f32[256]{0:T(256)S(1)} %get-tuple-element.3, f32[8]{0:T(128)S(1)} %broadcast_multiply_fusion.3, f32[8,256]{1,0:T(8,128)S(1)} %get-tuple-element.43, f32[256]{0:T(256)S(1)} %get-tuple-element.42), kind=kOutput, calls=%fused_computation.3 | convolution fusion | flops 16787456 | bytes 2239520 | tf_op jit(solution)/shard_map/dot_general | solution.py:49
  64.9 2.0 %convolution_bitcast_fusion.2 = f32[1,8,4096]{2,1,0:T(8,128)S(1)} fusion(bf16[4,256,4096]{2,1,0:T(8,128)(2,1)} %param.3, f32[256]{0:T(256)S(1)} %get-tuple-element.31, f32[256]{0:T(256)S(1)} %get-tuple-element.44, f32[8]{0:T(128)S(1)} %broadcast_multiply_fusion.2, f32[8,256]{1,0:T(8,128)S(1)} %get-tuple-element.41, f32[256]{0:T(256)S(1)} %get-tuple-element.40), kind=kOutput, calls=%fused_computation.2 | convolution fusion | flops 16787456 | bytes 2239520 | tf_op jit(solution)/shard_map/dot_general | solution.py:49
  66.9 0.2 fusion.57
  67.1 2.0 %convolution_bitcast_fusion.1 = f32[1,8,4096]{2,1,0:T(8,128)S(1)} fusion(bf16[4,256,4096]{2,1,0:T(8,128)(2,1)} %param.3, f32[256]{0:T(256)S(1)} %get-tuple-element.33, f32[256]{0:T(256)S(1)} %get-tuple-element.7, f32[8]{0:T(128)S(1)} %broadcast_multiply_fusion.1, f32[8,256]{1,0:T(8,128)S(1)} %get-tuple-element.39, f32[256]{0:T(256)S(1)} %get-tuple-element.38), kind=kOutput, calls=%fused_computation.1 | convolution fusion | flops 16787456 | bytes 2239520 | tf_op jit(solution)/shard_map/dot_general | solution.py:49
  69.1 2.0 %convolution_bitcast_fusion = f32[1,8,4096]{2,1,0:T(8,128)S(1)} fusion(bf16[4,256,4096]{2,1,0:T(8,128)(2,1)} %param.3, f32[256]{0:T(256)S(1)} %get-tuple-element.35, f32[256]{0:T(256)S(1)} %get-tuple-element.46, f32[8]{0:T(128)S(1)} %broadcast_multiply_fusion, f32[8,256]{1,0:T(8,128)S(1)} %get-tuple-element.37, f32[256]{0:T(256)S(1)} %get-tuple-element.36), kind=kOutput, calls=%fused_computation | convolution fusion | flops 16787456 | bytes 2239520 | tf_op jit(solution)/shard_map/dot_general | solution.py:49
  71.1 0.8 pad_maximum_fusion
  71.9 0.0 all-reduce.4.cloned.1.call-start
  72.0 2.6 %pad_maximum_fusion.3 = f32[4]{0:T(128)S(1)} fusion(f32[1]{0:T(128)} %bitcast.36, f32[1]{0:T(128)} %bitcast.35, f32[1]{0:T(128)} %bitcast.34, f32[1]{0:T(128)} %bitcast.33), kind=kLoop, calls=%fused_computation.95 | loop fusion | flops 12 | bytes 32 | tf_op jit(solution)/shard_map/stack | solution.py:54
  74.6 40.0 %all-reduce = (f32[4]{0:T(128)S(1)}, f32[4,8]{1,0:T(4,128)S(1)}) all-reduce(f32[4]{0:T(128)S(1)} %pad_maximum_fusion.3, f32[4,8]{1,0:T(4,128)S(1)} %pad_maximum_fusion.1), channel_id=1, replica_groups=mesh['dp'=8,'expert'=4] {'dp','expert'}, use_global_device_ids=true, to_apply=%region_32.0 | all-reduce | flops 36 | bytes 288 | tf_op jit(solution)/shard_map/psum | solution.py:53
  114.7 0.1 fusion.54
  114.8 0.6 pad_maximum_fusion.2
  115.4 34.5 %all-reduce.4.cloned.1.call-done = f32[4,8,512]{2,1,0:T(8,128)} async-done(((f32[4,8,512]{2,1,0:T(8,128)}), f32[4,8,512]{2,1,0:T(8,128)}) %all-reduce.4.cloned.1.call-update) | async-done | bytes 65552 | tf_op jit(solution)/shard_map/psum | solution.py:52
  149.9 1.5 copy.6
  (19 shorter events, 0.2 us)
Async XLA Ops:
  7.2 107.6 %reduce-scatter.2.cloned.1.call-start = ((), (), s32[]{:S(2)}) async-start(), calls=%async_computation.1 | async-start | bytes 589824 | tf_op jit(solution)/shard_map/reduce_scatter | solution.py:51
  71.9 78.0 %all-reduce.4.cloned.1.call-start = ((), (), s32[]{:S(2)}) async-start(), calls=%async_computation.2 | async-start | bytes 131072 | tf_op jit(solution)/shard_map/psum | solution.py:52
Sparse Core Ops, SparseCore 0:
  72.1 33.9 reduce-scatter.1
  115.0 34.9 all-reduce.3
where the time goes:
time: 159 us; the launch traced here: 158 us
  blocking collectives  82.1 us (52%)
  waiting for transfers between devices  34.6 us (22%)
  matrix products  17.3 us (11%)
  between operations  14.2 us (9%)
  other arithmetic  7.88 us (5%)
  local copies, waits for them, and re-layouts  2.23 us (1%)
    psum x1, blocking collectives, on_device(): lax.psum(local_counts(expert_ids[layer], experts), ('dp', 'expert'))  42 us
    psum x1, blocking collectives, on_device(): lax.psum((jnp.stack(prob_sums), jnp.stack(square_sums)), ('dp', 'expert'))  40 us
    psum x1, waiting for transfers between devices, on_device(): router_grad = lax.psum(columns, 'expert')  34.5 us
    dot_general x4, matrix products, on_device(): lax.dot_general(router_weight[layer], states, (((1,), (1,)), ((), ())), p...  9.21 us
    dot_general x4, matrix products, on_device(): term = jnp.dot(dlogits, states, preferred_element_type=jnp.float32)  8.06 us
  transfers between devices with their start and end apart: 2, of which 1 were waited for; matrix products, arithmetic and copies ran while one was open for 2% of the time, Pallas kernels for 0%

commit v1 on v0

--- a/solution.py
+++ b/solution.py
@@ -49,7 +49,7 @@
         term = jnp.dot(dlogits, states, preferred_element_type=jnp.float32)
         terms.append(term)
     columns = lax.psum_scatter(jnp.stack(terms), "dp", scatter_dimension=2, tiled=True)
-    router_grad = lax.psum(columns, "expert")
+    router_grad = jnp.sum(lax.all_gather(columns, "expert"), axis=0)
     prob_total, square_total = lax.psum(
         (jnp.stack(prob_sums), jnp.stack(square_sums)), ("dp", "expert")
     )

time: 159 us -> 138 us (0.87)
  waiting for transfers between devices: 34.6 us -> 0.02 us
  blocking collectives: 82.1 us -> 96.7 us
    psum x1 -> x0, waiting for transfers between devices: 34.5 us -> none  [on_device(): router_grad = lax.psum(columns, 'expert')]
    all_gather x0 -> x1, blocking collectives: none -> 14.6 us  [on_device(): router_grad = jnp.sum(lax.all_gather(columns, 'expert'), axis=0)]
  transfers between devices with their start and end apart: 2 -> 1, of which waited for: 1 -> 0; matrix products, arithmetic and copies ran while one was open for 2% -> 2% of each run, Pallas kernels for 0% -> 0%
where the time goes in v1:
time: 138 us; the launch traced here: 137 us
  blocking collectives  96.7 us (70%)
  matrix products  17.3 us (13%)
  between operations  14.1 us (10%)
  other arithmetic  8.53 us (6%)
    psum x1, blocking collectives, on_device(): lax.psum(local_counts(expert_ids[layer], experts), ('dp', 'expert'))  42 us
    psum x1, blocking collectives, on_device(): lax.psum((jnp.stack(prob_sums), jnp.stack(square_sums)), ('dp', 'expert'))  40 us
    all_gather x1, blocking collectives, on_device(): router_grad = jnp.sum(lax.all_gather(columns, 'expert'), axis=0)  14.6 us
    dot_general x4, matrix products, on_device(): lax.dot_general(router_weight[layer], states, (((1,), (1,)), ((), ())), p...  9.21 us
    dot_general x4, matrix products, on_device(): term = jnp.dot(dlogits, states, preferred_element_type=jnp.float32)  8.06 us
  transfers between devices with their start and end apart: 1, of which 0 were waited for; matrix products, arithmetic and copies ran while one was open for 2% of the time, Pallas kernels for 0%

profile of v1, /device:TPU:0, one launch (start us, length us, event | category | flops | bytes accessed | tf_op | source)
XLA Modules:
  0.0 137.4 jit_solution(5159721153701160064)
XLA Ops:
  7.2 0.0 reduce-scatter.2.cloned.1.call-start
  7.2 2.3 %fusion.65 = (f32[256]{0:T(256)S(1)}, f32[8,256]{1,0:T(8,128)S(1)}) fusion(bf16[4,256,4096]{2,1,0:T(8,128)(2,1)} %param.3, bf16[4,8,4096]{2,1,0:T(8,128)(2,1)} %param.4), kind=kOutput, calls=%fused_computation.112 | convolution fusion | flops 16779008 | bytes 2171904 | tf_op jit(solution)/shard_map/dot_general | solution.py:30
  9.5 2.3 %fusion.66 = (f32[256]{0:T(256)S(1)}, f32[8,256]{1,0:T(8,128)S(1)}) fusion(bf16[4,256,4096]{2,1,0:T(8,128)(2,1)} %param.3, bf16[4,8,4096]{2,1,0:T(8,128)(2,1)} %param.4), kind=kOutput, calls=%fused_computation.113 | convolution fusion | flops 16779008 | bytes 2171904 | tf_op jit(solution)/shard_map/dot_general | solution.py:30
  11.8 2.3 %fusion.63 = (f32[256]{0:T(256)S(1)}, f32[8,256]{1,0:T(8,128)S(1)}) fusion(bf16[4,256,4096]{2,1,0:T(8,128)(2,1)} %param.3, bf16[4,8,4096]{2,1,0:T(8,128)(2,1)} %param.4), kind=kOutput, calls=%fused_computation.110 | convolution fusion | flops 16779008 | bytes 2171904 | tf_op jit(solution)/shard_map/dot_general | solution.py:30
  14.1 0.7 slice_bitcast_fusion.3
  14.9 0.1 convert_reduce_fusion.6
  15.0 0.1 convert_reduce_fusion.7
  15.1 0.1 convert_reduce_fusion.4
  15.2 0.1 convert_reduce_fusion.5
  15.4 0.1 convert_reduce_fusion
  15.5 0.1 convert_reduce_fusion.1
  15.6 0.1 convert_reduce_fusion.2
  15.7 0.1 convert_reduce_fusion.3
  15.9 2.3 %fusion.64 = (f32[256]{0:T(256)S(1)}, f32[8,256]{1,0:T(8,128)S(1)}) fusion(bf16[4,256,4096]{2,1,0:T(8,128)(2,1)} %param.3, bf16[4,8,4096]{2,1,0:T(8,128)(2,1)} %param.4), kind=kOutput, calls=%fused_computation.111 | convolution fusion | flops 16779008 | bytes 2171904 | tf_op jit(solution)/shard_map/dot_general | solution.py:30
  18.2 42.0 %all-reduce.1 = (f32[8]{0:T(128)S(1)}, f32[8]{0:T(128)S(1)}, f32[8]{0:T(128)S(1)}, f32[8]{0:T(128)S(1)}) all-reduce(f32[8]{0:T(128)S(1)} %add.44, f32[8]{0:T(128)S(1)} %add.42, f32[8]{0:T(128)S(1)} %add.40, f32[8]{0:T(128)S(1)} %add.38), channel_id=1, replica_groups=mesh['dp'=8,'expert'=4] {'dp','expert'}, use_global_device_ids=true, to_apply=%region_18.0 | all-reduce | flops 32 | bytes 256 | tf_op jit(solution)/shard_map/psum | solution.py:42
  60.2 0.6 multiply_reduce_fusion.6
  60.8 0.7 multiply_reduce_fusion.7
  61.5 0.6 multiply_reduce_fusion.4
  62.1 0.6 multiply_reduce_fusion.5
  62.7 0.2 fusion.55
  62.9 2.0 %convolution_bitcast_fusion.3 = f32[1,8,4096]{2,1,0:T(8,128)S(1)} fusion(bf16[4,256,4096]{2,1,0:T(8,128)(2,1)} %param.3, f32[256]{0:T(256)S(1)} %get-tuple-element.29, f32[256]{0:T(256)S(1)} %get-tuple-element.3, f32[8]{0:T(128)S(1)} %broadcast_multiply_fusion.3, f32[8,256]{1,0:T(8,128)S(1)} %get-tuple-element.43, f32[256]{0:T(256)S(1)} %get-tuple-element.42), kind=kOutput, calls=%fused_computation.3 | convolution fusion | flops 16787456 | bytes 2239520 | tf_op jit(solution)/shard_map/dot_general | solution.py:49
  64.9 2.0 %convolution_bitcast_fusion.2 = f32[1,8,4096]{2,1,0:T(8,128)S(1)} fusion(bf16[4,256,4096]{2,1,0:T(8,128)(2,1)} %param.3, f32[256]{0:T(256)S(1)} %get-tuple-element.31, f32[256]{0:T(256)S(1)} %get-tuple-element.44, f32[8]{0:T(128)S(1)} %broadcast_multiply_fusion.2, f32[8,256]{1,0:T(8,128)S(1)} %get-tuple-element.41, f32[256]{0:T(256)S(1)} %get-tuple-element.40), kind=kOutput, calls=%fused_computation.2 | convolution fusion | flops 16787456 | bytes 2239520 | tf_op jit(solution)/shard_map/dot_general | solution.py:49
  66.9 0.2 fusion.57
  67.0 2.0 %convolution_bitcast_fusion.1 = f32[1,8,4096]{2,1,0:T(8,128)S(1)} fusion(bf16[4,256,4096]{2,1,0:T(8,128)(2,1)} %param.3, f32[256]{0:T(256)S(1)} %get-tuple-element.33, f32[256]{0:T(256)S(1)} %get-tuple-element.7, f32[8]{0:T(128)S(1)} %broadcast_multiply_fusion.1, f32[8,256]{1,0:T(8,128)S(1)} %get-tuple-element.39, f32[256]{0:T(256)S(1)} %get-tuple-element.38), kind=kOutput, calls=%fused_computation.1 | convolution fusion | flops 16787456 | bytes 2239520 | tf_op jit(solution)/shard_map/dot_general | solution.py:49
  69.1 2.0 %convolution_bitcast_fusion = f32[1,8,4096]{2,1,0:T(8,128)S(1)} fusion(bf16[4,256,4096]{2,1,0:T(8,128)(2,1)} %param.3, f32[256]{0:T(256)S(1)} %get-tuple-element.35, f32[256]{0:T(256)S(1)} %get-tuple-element.46, f32[8]{0:T(128)S(1)} %broadcast_multiply_fusion, f32[8,256]{1,0:T(8,128)S(1)} %get-tuple-element.37, f32[256]{0:T(256)S(1)} %get-tuple-element.36), kind=kOutput, calls=%fused_computation | convolution fusion | flops 16787456 | bytes 2239520 | tf_op jit(solution)/shard_map/dot_general | solution.py:49
  71.1 0.8 pad_maximum_fusion
  71.9 2.6 %pad_maximum_fusion.3 = f32[4]{0:T(128)S(1)} fusion(f32[1]{0:T(128)} %bitcast.37, f32[1]{0:T(128)} %bitcast.36, f32[1]{0:T(128)} %bitcast.35, f32[1]{0:T(128)} %bitcast.34), kind=kLoop, calls=%fused_computation.95 | loop fusion | flops 12 | bytes 32 | tf_op jit(solution)/shard_map/stack | solution.py:54
  74.5 40.0 %all-reduce = (f32[4]{0:T(128)S(1)}, f32[4,8]{1,0:T(4,128)S(1)}) all-reduce(f32[4]{0:T(128)S(1)} %pad_maximum_fusion.3, f32[4,8]{1,0:T(4,128)S(1)} %pad_maximum_fusion.1), channel_id=1, replica_groups=mesh['dp'=8,'expert'=4] {'dp','expert'}, use_global_device_ids=true, to_apply=%region_32.0 | all-reduce | flops 36 | bytes 288 | tf_op jit(solution)/shard_map/psum | solution.py:53
  114.6 0.1 fusion.54
  114.7 0.6 pad_maximum_fusion.2
  115.3 14.6 %all-gather = f32[16,8,512]{2,1,0:T(8,128)S(1)} all-gather(f32[4,8,512]{2,1,0:T(8,128)} %reduce-scatter.2.cloned.1.call-done), channel_id=2, replica_groups=mesh['dp'=8,'expert'=4] {'expert'}, dimensions={0}, use_global_device_ids=true | all-gather | bytes 327680 | tf_op jit(solution)/shard_map/all_gather | solution.py:52
  129.9 0.6 reduce_sum.250
  (17 shorter events, 0.1 us)
Async XLA Ops:
  7.2 108.1 %reduce-scatter.2.cloned.1.call-start = ((), (), s32[]{:S(2)}) async-start(), calls=%async_computation.1 | async-start | bytes 589824 | tf_op jit(solution)/shard_map/reduce_scatter | solution.py:51
Sparse Core Ops, SparseCore 0:
  72.0 33.9 reduce-scatter.1
